TPU v7x, 32 devices: a whole 2x2x4 slice. The times are simulated.
32 devices in a mesh: ep: 8 (over y, x, core), tp: 4 (over z).
Axes of the slice: x: 2, y: 2, z: 4, core: 2. Of those that a mesh axis runs over, the one named last changes fastest.
Arguments:
- tokens: bfloat16 [256, 4096], P('ep', 'tp'), may hold values from -6 to 6
- norm_gains: float32 [2, 4096], replicated, may hold values from 0.1 to 1.9
- router: bfloat16 [2, 4096, 16], replicated, as said below
- w_gate: bfloat16 [2, 16, 4096, 768], P(None, 'ep', None, 'tp'), may hold values from -0.09375 to 0.09375
- w_up: bfloat16 [2, 16, 4096, 768], P(None, 'ep', None, 'tp'), may hold values from -0.09375 to 0.09375
- w_down: bfloat16 [2, 16, 768, 4096], P(None, 'ep', 'tp'), may hold values from -0.21875 to 0.21875
- expert_ids: int32 [2, 256, 8], P(None, 'ep'), may hold values from 0 to 15, all different within a row; in each aligned block of 32 rows (0 to 31, 32 to 63, ...) at most 32 rows name the same one
Outputs:
- hidden_out: bfloat16 [256, 4096], P('ep', 'tp')
Inputs may be any that keep to these rules, and one draw needn't show every extreme that they name: `expert_ids`: each entry names an expert of 0 to 15; the 8 entries of a token differ; among the 32 tokens of one ep index in one layer no expert is named more than 32 times, and in some such blocks one is named exactly 32 times. `router`: entries of order 2 / sqrt(4096); all columns of a layer may share a common added vector with entries of order 50 / sqrt(4096).
All inputs are finite; a program needn't handle non-finite values.
Results may differ from a plain program's by a relative error of at most 0.02.
Values may be sent and summed in bfloat16 or wider, within the bound.
A program may use at most 64 MiB of HBM per device.

v0:
```python
import jax
import jax.numpy as jnp
from jax import lax
from jax.sharding import PartitionSpec as P

TOP = 8
LAYERS = 2
norm_eps = 1e-06


def body(tokens, norm_gains, router, w_gate, w_up, w_down, expert_ids):
    n_tp = lax.axis_size("tp")
    n_ep = lax.axis_size("ep")
    local_width = tokens.shape[1]
    full_width = local_width * n_tp
    rows_dev = tokens.shape[0]
    local_exp = w_gate.shape[1]
    experts = local_exp * n_ep
    capacity = 2 * rows_dev * TOP // experts
    current = tokens
    for layer_idx in range(LAYERS):
        gain = norm_gains[layer_idx]
        weight = router[layer_idx]
        ids = expert_ids[layer_idx]
        normed = None
        whole = lax.all_gather(current, "tp", axis=1, tiled=True)
        wide_rows = whole.astype(jnp.float32)
        square_sum = jnp.sum(wide_rows * wide_rows, axis=1)
        scaled = (wide_rows * gain[None, :]).astype(jnp.bfloat16)
        raw_logits = jnp.dot(scaled, weight, preferred_element_type=jnp.float32)
        inverse = lax.rsqrt(square_sum / full_width + norm_eps)
        normed = (scaled.astype(jnp.float32) * inverse[:, None]).astype(jnp.bfloat16)
        logits = raw_logits * inverse[:, None]
        choose = ids[:, :, None] == lax.iota(jnp.int32, experts)[None, None, :]
        picked = jnp.sum(jnp.where(choose, logits[:, None, :], 0.0), axis=-1)
        gate_probs = jax.nn.softmax(picked, axis=-1)
        onehot = choose.reshape(rows_dev * TOP, experts).astype(jnp.int32)
        earlier = jnp.cumsum(onehot, axis=0) - onehot
        slot_index = jnp.sum(earlier * onehot, axis=1).reshape(rows_dev, TOP)
        slot_key = ids * capacity + slot_index
        slot_hits = slot_key[None, :, :] == lax.iota(jnp.int32, experts * capacity)[:, None, None]
        route_matrix = jnp.any(slot_hits, axis=-1).astype(jnp.bfloat16)
        combine_matrix = jnp.sum(jnp.where(slot_hits, gate_probs[None, :, :], 0.0), axis=-1).T
        outgoing = jnp.dot(route_matrix, normed, preferred_element_type=jnp.float32).astype(
            jnp.bfloat16
        )
        outgoing = outgoing.reshape(n_ep, local_exp * capacity, full_width)
        incoming = lax.all_to_all(outgoing, "ep", split_axis=0, concat_axis=0, tiled=True)
        arrived = incoming.reshape(n_ep, local_exp, capacity, full_width).transpose(1, 0, 2, 3)
        arrived = arrived.reshape(local_exp, n_ep * capacity, full_width)
        gate_proj = jnp.einsum(
            "erd,edf->erf", arrived, w_gate[layer_idx], preferred_element_type=jnp.float32
        )
        up_proj = jnp.einsum(
            "erd,edf->erf", arrived, w_up[layer_idx], preferred_element_type=jnp.float32
        )
        inner = (jax.nn.silu(gate_proj) * up_proj).astype(jnp.bfloat16)
        down_local = w_down[layer_idx]

        def project():
            down_piece = lax.slice_in_dim(down_local, 0, local_width * lax.axis_size("tp"), axis=2)
            return jnp.einsum("erf,efd->der", inner, down_piece, preferred_element_type=jnp.float32)

        summed = lax.psum_scatter(
            project().astype(jnp.bfloat16), "tp", scatter_dimension=0, tiled=True
        ).astype(jnp.float32)
        out_rows = summed.astype(jnp.bfloat16).reshape(local_width, local_exp, n_ep, capacity)
        out_rows = out_rows.transpose(2, 1, 3, 0).reshape(n_ep, local_exp * capacity, local_width)
        returned = lax.all_to_all(out_rows, "ep", split_axis=0, concat_axis=0, tiled=True)
        returned = returned.reshape(experts * capacity, local_width).astype(jnp.float32)
        moe_out = jnp.dot(combine_matrix, returned, precision=lax.Precision.HIGHEST)
        current = (current.astype(jnp.float32) + moe_out).astype(jnp.bfloat16)
    return current


def solution(mesh):
    in_specs = (
        P("ep", "tp"),
        P(),
        P(),
        P(None, "ep", None, "tp"),
        P(None, "ep", None, "tp"),
        P(None, "ep", "tp", None),
        P(None, "ep", None),
    )
    out_specs = P("ep", "tp")
    return jax.shard_map(body, mesh=mesh, in_specs=in_specs, out_specs=out_specs, check_vma=False)
```

profile of v0, /device:TPU:0, one launch (start us, length us, event | category | flops | bytes accessed | tf_op | source)
XLA Modules:
  0.0 376.2 jit_solution(15348728780867839647)
XLA Ops:
  6.5 0.7 fusion.79
  7.3 0.1 eq.102
  7.4 0.1 eq.98
  7.5 0.6 reduce-window.14
  8.1 0.2 slice_reduce_fusion.1
  8.3 0.1 fusion.69
  8.4 0.1 reshape.147
  8.5 0.2 fusion.41
  8.8 0.9 fusion.78
  9.6 15.9 %all_gather.6 = bf16[32,4096]{1,0:T(8,128)(2,1)S(1)} all-gather(bf16[32,1024]{1,0:T(8,128)(2,1)} %param.7), channel_id=1, replica_groups=mesh['ep'=8,'tp'=4] {'tp'}, dimensions={1}, use_global_device_ids=true | all-gather | bytes 327680 | tf_op jit(solution)/shard_map/all_gather | solution.py:26
  25.5 0.2 fusion.37
  25.7 1.3 convolution_convert_fusion.3
  27.0 52.8 %all_to_all.20 = bf16[8,64,4096]{2,1,0:T(8,128)(2,1)S(1)} all-to-all(bf16[8,64,4096]{2,1,0:T(8,128)(2,1)S(1)} %bitcast.120), channel_id=1, replica_groups=mesh['ep'=8,'tp'=4] {'ep'}, dimensions={0} | all-to-all | bytes 8388608 | tf_op jit(solution)/shard_map/all_to_all | solution.py:48
  79.8 0.5 copy.30
  80.3 2.0 copy-done
  82.3 1.5 fusion.10
  83.9 8.8 %fusion = bf16[4096,2,256]{0,2,1:T(8,128)(2,1)} fusion(bf16[2,2,192,4096]{3,2,1,0:T(8,128)(2,1)} %param.12, bf16[2,256,4096]{2,1,0:T(8,128)(2,1)} %bitcast.125, bf16[2,2,4096,192]{2,3,1,0:T(8,128)(2,1)} %param.11, f32[2,256,192]{1,2,0:T(8,128)S(1)} %fusion.10), kind=kOutput, calls=%fused_computation.4 | convolution fusion | flops 1613299712 | bytes 15073280 | tf_op jit(solution)/shard_map/erf,efd->der/dot_general | solution.py:62
  92.8 0.1 eq.118
  92.8 0.1 eq.114
  92.9 0.6 reduce-window.16
  93.5 0.2 slice_reduce_fusion
  93.8 0.1 fusion.66
  93.9 0.1 reshape.155
  94.0 0.2 convolution_multiply_fusion.1
  94.1 75.1 %reduce-scatter.3.cloned.1.call-done = bf16[1024,2,256]{0,2,1:T(8,128)(2,1)} async-done(((bf16[4096,2,256]{0,2,1:T(8,128)(2,1)}), bf16[1024,2,256]{0,2,1:T(8,128)(2,1)}) %reduce-scatter.3.cloned.1.call-update) | async-done | bytes 1048592 | tf_op jit(solution)/shard_map/reduce_scatter | solution.py:64
  169.3 2.3 copy.31
  171.6 3.6 all-to-all-start.1
  175.4 0.1 copy.29
  175.4 0.2 fusion.40
  175.7 0.2 select_reduce_fusion.1
  175.9 14.7 %all-to-all-done.1 = bf16[8,64,1024]{2,1,0:T(8,128)(2,1)S(1)} async-done(((bf16[8,64,1024]{2,1,0:T(8,128)(2,1)}), bf16[8,64,1024]{2,1,0:T(8,128)(2,1)S(1)}, u32[]{:S(2)}, u32[]{:S(2)}) %all-to-all-start.1) | async-done | bytes 1048608 | tf_op jit(solution)/shard_map/all_to_all | solution.py:69
  190.6 0.6 fusion.30
  191.2 14.4 %all_gather.7 = bf16[32,4096]{1,0:T(8,128)(2,1)S(1)} all-gather(bf16[32,1024]{1,0:T(8,128)(2,1)S(1)} %fusion.30), channel_id=1, replica_groups=mesh['ep'=8,'tp'=4] {'tp'}, dimensions={1}, use_global_device_ids=true | all-gather | bytes 327680 | tf_op jit(solution)/shard_map/all_gather | solution.py:26
  205.6 0.2 fusion.39
  205.8 1.3 convolution_convert_fusion.1
  207.1 51.8 %all_to_all.21 = bf16[8,64,4096]{2,1,0:T(8,128)(2,1)S(1)} all-to-all(bf16[8,64,4096]{2,1,0:T(8,128)(2,1)S(1)} %bitcast.122), channel_id=1, replica_groups=mesh['ep'=8,'tp'=4] {'ep'}, dimensions={0} | all-to-all | bytes 8388608 | tf_op jit(solution)/shard_map/all_to_all | solution.py:48
  258.9 0.5 copy.36
  259.4 2.0 copy-done.1
  261.4 1.5 fusion.5
  262.9 8.8 %fusion.1 = bf16[4096,2,256]{0,2,1:T(8,128)(2,1)} fusion(bf16[2,2,192,4096]{3,2,1,0:T(8,128)(2,1)} %param.12, bf16[2,256,4096]{2,1,0:T(8,128)(2,1)} %bitcast.127, bf16[2,2,4096,192]{2,3,1,0:T(8,128)(2,1)} %param.11, f32[2,256,192]{1,2,0:T(8,128)S(1)} %fusion.5), kind=kOutput, calls=%fused_computation.5 | convolution fusion | flops 1613299712 | bytes 15073280 | tf_op jit(solution)/shard_map/erf,efd->der/dot_general | solution.py:62
  271.7 75.0 %reduce-scatter.5.cloned.1.call-done = bf16[1024,2,256]{0,2,1:T(8,128)(2,1)} async-done(((bf16[4096,2,256]{0,2,1:T(8,128)(2,1)}), bf16[1024,2,256]{0,2,1:T(8,128)(2,1)}) %reduce-scatter.5.cloned.1.call-update) | async-done | bytes 1048592 | tf_op jit(solution)/shard_map/reduce_scatter | solution.py:64
  346.7 2.3 copy.37
  349.0 3.7 all-to-all-start.3
  352.7 0.2 convolution_multiply_fusion
  353.0 0.1 copy.35
  353.1 0.2 select_reduce_fusion
  353.3 14.8 %all-to-all-done.3 = bf16[8,64,1024]{2,1,0:T(8,128)(2,1)S(1)} async-done(((bf16[8,64,1024]{2,1,0:T(8,128)(2,1)}), bf16[8,64,1024]{2,1,0:T(8,128)(2,1)S(1)}, u32[]{:S(2)}, u32[]{:S(2)}) %all-to-all-start.3) | async-done | bytes 1048608 | tf_op jit(solution)/shard_map/all_to_all | solution.py:69
  368.1 1.2 fusion.31
  (40 shorter events, 0.6 us)
Async XLA Ops:
  6.5 162.8 %reduce-scatter.3.cloned.1.call-start = ((), (), s32[]{:S(2)}) async-start(), calls=%async_computation.6 | async-start | bytes 5242880 | tf_op jit(solution)/shard_map/reduce_scatter | solution.py:64
  27.0 55.3 %slice-start = ((s8[6291456]{0:T(1024)(128)(4,1)}), s8[4194304]{0:T(1024)(128)(4,1)S(1)}, s32[]{:S(2)}) async-start(s8[6291456]{0:T(1024)(128)(4,1)} %bitcast.136), calls=%async_computation.8 | async-start | bytes 8388608
  79.8 2.5 slice-start.1
  80.3 2.0 copy-start
  92.6 1.3 copy-start.3
  92.6 98.0 %copy-start.2 = (bf16[32,1024]{1,0:T(8,128)(2,1)S(1)}, bf16[32,1024]{1,0:T(8,128)(2,1)}, u32[]{:S(2)}) copy-start(bf16[32,1024]{1,0:T(8,128)(2,1)} %param.7) | copy-start | bytes 196612
  171.6 19.0 %all-to-all-start.1 = ((bf16[8,64,1024]{2,1,0:T(8,128)(2,1)}), bf16[8,64,1024]{2,1,0:T(8,128)(2,1)S(1)}, u32[]{:S(2)}, u32[]{:S(2)}) async-start(bf16[8,64,1024]{2,1,0:T(8,128)(2,1)} %bitcast.16), calls=%async_computation.2 | async-start | bytes 2097152 | tf_op jit(solution)/shard_map/all_to_all | solution.py:69
  175.2 171.5 %reduce-scatter.5.cloned.1.call-start = ((), (), s32[]{:S(2)}) async-start(), calls=%async_computation.7 | async-start | bytes 5242880 | tf_op jit(solution)/shard_map/reduce_scatter | solution.py:64
  207.1 54.3 %slice-start.2 = ((s8[6291456]{0:T(1024)(128)(4,1)}), s8[4194304]{0:T(1024)(128)(4,1)S(1)}, s32[]{:S(2)}) async-start(s8[6291456]{0:T(1024)(128)(4,1)} %bitcast.138), calls=%async_computation.10 | async-start | bytes 8388608
  258.9 2.5 slice-start.3
  259.4 2.0 copy-start.1
  349.0 19.0 %all-to-all-start.3 = ((bf16[8,64,1024]{2,1,0:T(8,128)(2,1)}), bf16[8,64,1024]{2,1,0:T(8,128)(2,1)S(1)}, u32[]{:S(2)}, u32[]{:S(2)}) async-start(bf16[8,64,1024]{2,1,0:T(8,128)(2,1)} %bitcast.34), calls=%async_computation.5 | async-start | bytes 2097152 | tf_op jit(solution)/shard_map/all_to_all | solution.py:69
Sparse Core Ops, SparseCore 0:
  92.8 76.4 reduce-scatter.2
  271.8 74.8 reduce-scatter.4
where the time goes:
time: 377 us; the launch traced here: 376 us
  waiting for transfers between devices  180 us (48%)
  blocking collectives  135 us (36%)
  matrix products  25.5 us (7%)
  between operations  13.6 us (4%)
  local copies, waits for them, and re-layouts  12.3 us (3%)
  starting transfers between devices  7.32 us (2%)
    reduce_scatter x2, waiting for transfers between devices, body(): lax.psum_scatter(project().astype(jnp.bfloat16), 'tp', scatter_dimension=...  150 us
    all_to_all x2, blocking collectives, body(): lax.all_to_all(outgoing, 'ep', split_axis=0, concat_axis=0, tiled=True)  105 us
    all_gather x2, blocking collectives, body(): whole = lax.all_gather(current, 'tp', axis=1, tiled=True)  30.2 us
    all_to_all x2, waiting for transfers between devices, body(): lax.all_to_all(out_rows, 'ep', split_axis=0, concat_axis=0, tiled=True)  29.5 us
    dot_general x2, matrix products, project(): jnp.einsum('erf,efd->der', inner, down_piece, preferred_element_type=jnp....  17.6 us
  transfers between devices with their start and end apart: 4, of which 4 were waited for; matrix products, arithmetic and copies ran while one was open for 1% of the time, Pallas kernels for 0%

commit v1 on v0

--- a/solution.py
+++ b/solution.py
@@ -23,7 +23,7 @@
         weight = router[layer_idx]
         ids = expert_ids[layer_idx]
         normed = None
-        whole = lax.all_gather(current, "tp", axis=1, tiled=True)
+        whole = jnp.concatenate(lax.all_gather(current, "tp"), axis=1)
         wide_rows = whole.astype(jnp.float32)
         square_sum = jnp.sum(wide_rows * wide_rows, axis=1)
         scaled = (wide_rows * gain[None, :]).astype(jnp.bfloat16)

time: 377 us -> 378 us (level)
  no operation moved by 1% of the time
where the time goes in v1:
time: 378 us
  waiting for transfers between devices  179 us (47%)
  blocking collectives  135 us (36%)
  matrix products  25.5 us (7%)
  local copies, waits for them, and re-layouts  13.8 us (4%)
  between operations  13.6 us (4%)
  starting transfers between devices  7.35 us (2%)
  other arithmetic  3.83 us (1%)
    reduce_scatter x2, waiting for transfers between devices, body(): lax.psum_scatter(project().astype(jnp.bfloat16), 'tp', scatter_dimension=...  150 us
    all_to_all x2, blocking collectives, body(): lax.all_to_all(outgoing, 'ep', split_axis=0, concat_axis=0, tiled=True)  105 us
    all_gather x2, blocking collectives, body(): whole = jnp.concatenate(lax.all_gather(current, 'tp'), axis=1)  30.2 us
    all_to_all x2, waiting for transfers between devices, body(): lax.all_to_all(out_rows, 'ep', split_axis=0, concat_axis=0, tiled=True)  28.5 us
    dot_general x2, matrix products, project(): jnp.einsum('erf,efd->der', inner, down_piece, preferred_element_type=jnp....  17.6 us
  transfers between devices with their start and end apart: 4, of which 4 were waited for; matrix products, arithmetic and copies ran while one was open for 1% of the time, Pallas kernels for 0%

profile of v1, /device:TPU:0, one launch (start us, length us, event | category | flops | bytes accessed | tf_op | source)
XLA Modules:
  0.0 377.8 jit_solution(2787158290172367113)
XLA Ops:
  6.5 0.7 fusion.74
  7.3 0.1 eq.98
  7.4 0.1 eq.102
  7.5 15.9 %all-gather = bf16[128,1024]{1,0:T(8,128)(2,1)S(1)} all-gather(bf16[32,1024]{1,0:T(8,128)(2,1)} %param.7), channel_id=2, replica_groups=mesh['ep'=8,'tp'=4] {'tp'}, dimensions={0}, use_global_device_ids=true | all-gather | bytes 327680 | tf_op jit(solution)/shard_map/all_gather | solution.py:26
  23.4 0.9 slice_reduce_fusion.3
  24.4 0.2 multiply_reduce_fusion.1
  24.6 0.6 reduce-window.14
  25.1 0.2 slice_reduce_fusion.1
  25.4 0.1 fusion.63
  25.6 0.2 fusion.37
  25.8 0.4 fusion.73
  26.2 0.3 copy.53
  26.5 1.3 convolution_convert_fusion.3
  27.9 52.8 %all_to_all.20 = bf16[8,64,4096]{2,1,0:T(8,128)(2,1)S(1)} all-to-all(bf16[8,64,4096]{2,1,0:T(8,128)(2,1)S(1)} %bitcast.140), channel_id=1, replica_groups=mesh['ep'=8,'tp'=4] {'ep'}, dimensions={0} | all-to-all | bytes 8388608 | tf_op jit(solution)/shard_map/all_to_all | solution.py:48
  80.7 0.5 copy.36
  81.2 2.0 copy-done
  83.2 1.5 fusion.10
  84.7 8.8 %fusion = bf16[4096,2,256]{0,2,1:T(8,128)(2,1)} fusion(bf16[2,2,192,4096]{3,2,1,0:T(8,128)(2,1)} %param.12, bf16[2,256,4096]{2,1,0:T(8,128)(2,1)} %bitcast.145, bf16[2,2,4096,192]{2,3,1,0:T(8,128)(2,1)} %param.11, f32[2,256,192]{1,2,0:T(8,128)S(1)} %fusion.10), kind=kOutput, calls=%fused_computation.4 | convolution fusion | flops 1613299712 | bytes 15073280 | tf_op jit(solution)/shard_map/erf,efd->der/dot_general | solution.py:62
  93.6 0.1 eq.114
  93.9 0.6 copy-done.3
  94.4 0.2 convolution_multiply_fusion.1
  94.8 75.3 %reduce-scatter.3.cloned.1.call-done = bf16[1024,2,256]{0,2,1:T(8,128)(2,1)} async-done(((bf16[4096,2,256]{0,2,1:T(8,128)(2,1)}), bf16[1024,2,256]{0,2,1:T(8,128)(2,1)}) %reduce-scatter.3.cloned.1.call-update) | async-done | bytes 1048592 | tf_op jit(solution)/shard_map/reduce_scatter | solution.py:64
  170.1 2.3 copy.37
  172.4 3.7 all-to-all-start.1
  176.1 0.6 reduce-window.16
  176.7 0.2 slice_reduce_fusion
  177.0 0.1 fusion.60
  177.2 0.2 fusion.36
  177.4 0.2 select_reduce_fusion.1
  177.6 13.8 %all-to-all-done.1 = bf16[8,64,1024]{2,1,0:T(8,128)(2,1)S(1)} async-done(((bf16[8,64,1024]{2,1,0:T(8,128)(2,1)}), bf16[8,64,1024]{2,1,0:T(8,128)(2,1)S(1)}, u32[]{:S(2)}, u32[]{:S(2)}) %all-to-all-start.1) | async-done | bytes 1048608 | tf_op jit(solution)/shard_map/all_to_all | solution.py:69
  191.5 0.6 fusion.30
  192.1 14.4 %all-gather.1 = bf16[128,1024]{1,0:T(8,128)(2,1)S(1)} all-gather(bf16[32,1024]{1,0:T(8,128)(2,1)S(1)} %fusion.30), channel_id=3, replica_groups=mesh['ep'=8,'tp'=4] {'tp'}, dimensions={0}, use_global_device_ids=true | all-gather | bytes 327680 | tf_op jit(solution)/shard_map/all_gather | solution.py:26
  206.5 0.2 multiply_reduce_fusion
  206.7 0.4 fusion.72
  207.1 0.3 copy.55
  207.4 1.3 convolution_convert_fusion.1
  208.7 51.8 %all_to_all.21 = bf16[8,64,4096]{2,1,0:T(8,128)(2,1)S(1)} all-to-all(bf16[8,64,4096]{2,1,0:T(8,128)(2,1)S(1)} %bitcast.141), channel_id=1, replica_groups=mesh['ep'=8,'tp'=4] {'ep'}, dimensions={0} | all-to-all | bytes 8388608 | tf_op jit(solution)/shard_map/all_to_all | solution.py:48
  260.5 0.5 copy.44
  261.0 2.0 copy-done.1
  263.0 1.5 fusion.5
  264.5 8.8 %fusion.1 = bf16[4096,2,256]{0,2,1:T(8,128)(2,1)} fusion(bf16[2,2,192,4096]{3,2,1,0:T(8,128)(2,1)} %param.12, bf16[2,256,4096]{2,1,0:T(8,128)(2,1)} %bitcast.147, bf16[2,2,4096,192]{2,3,1,0:T(8,128)(2,1)} %param.11, f32[2,256,192]{1,2,0:T(8,128)S(1)} %fusion.5), kind=kOutput, calls=%fused_computation.5 | convolution fusion | flops 1613299712 | bytes 15073280 | tf_op jit(solution)/shard_map/erf,efd->der/dot_general | solution.py:62
  273.3 75.0 %reduce-scatter.5.cloned.1.call-done = bf16[1024,2,256]{0,2,1:T(8,128)(2,1)} async-done(((bf16[4096,2,256]{0,2,1:T(8,128)(2,1)}), bf16[1024,2,256]{0,2,1:T(8,128)(2,1)}) %reduce-scatter.5.cloned.1.call-update) | async-done | bytes 1048592 | tf_op jit(solution)/shard_map/reduce_scatter | solution.py:64
  348.4 2.3 copy.45
  350.7 3.7 all-to-all-start.3
  354.4 0.2 convolution_multiply_fusion
  354.8 0.2 select_reduce_fusion
  355.0 14.7 %all-to-all-done.3 = bf16[8,64,1024]{2,1,0:T(8,128)(2,1)S(1)} async-done(((bf16[8,64,1024]{2,1,0:T(8,128)(2,1)}), bf16[8,64,1024]{2,1,0:T(8,128)(2,1)S(1)}, u32[]{:S(2)}, u32[]{:S(2)}) %all-to-all-start.3) | async-done | bytes 1048608 | tf_op jit(solution)/shard_map/all_to_all | solution.py:69
  369.7 1.2 fusion.31
  (50 shorter events, 1.3 us)
Async XLA Ops:
  6.5 163.6 %reduce-scatter.3.cloned.1.call-start = ((), (), s32[]{:S(2)}) async-start(), calls=%async_computation.6 | async-start | bytes 5242880 | tf_op jit(solution)/shard_map/reduce_scatter | solution.py:64
  27.9 55.3 %slice-start = ((s8[6291456]{0:T(1024)(128)(4,1)}), s8[4194304]{0:T(1024)(128)(4,1)S(1)}, s32[]{:S(2)}) async-start(s8[6291456]{0:T(1024)(128)(4,1)} %bitcast.164), calls=%async_computation.8 | async-start | bytes 8388608
  80.7 2.5 slice-start.1
  81.2 2.0 copy-start
  93.5 0.9 copy-start.3
  93.5 98.0 %copy-start.2 = (bf16[32,1024]{1,0:T(8,128)(2,1)S(1)}, bf16[32,1024]{1,0:T(8,128)(2,1)}, u32[]{:S(2)}) copy-start(bf16[32,1024]{1,0:T(8,128)(2,1)} %param.7) | copy-start | bytes 196612
  172.4 19.0 %all-to-all-start.1 = ((bf16[8,64,1024]{2,1,0:T(8,128)(2,1)}), bf16[8,64,1024]{2,1,0:T(8,128)(2,1)S(1)}, u32[]{:S(2)}, u32[]{:S(2)}) async-start(bf16[8,64,1024]{2,1,0:T(8,128)(2,1)} %bitcast.20), calls=%async_computation.2 | async-start | bytes 2097152 | tf_op jit(solution)/shard_map/all_to_all | solution.py:69
  176.1 172.3 %reduce-scatter.5.cloned.1.call-start = ((), (), s32[]{:S(2)}) async-start(), calls=%async_computation.7 | async-start | bytes 5242880 | tf_op jit(solution)/shard_map/reduce_scatter | solution.py:64
  208.7 54.3 %slice-start.2 = ((s8[6291456]{0:T(1024)(128)(4,1)}), s8[4194304]{0:T(1024)(128)(4,1)S(1)}, s32[]{:S(2)}) async-start(s8[6291456]{0:T(1024)(128)(4,1)} %bitcast.166), calls=%async_computation.10 | async-start | bytes 8388608
  260.5 2.5 slice-start.3
  261.0 2.0 copy-start.1
  350.7 19.0 %all-to-all-start.3 = ((bf16[8,64,1024]{2,1,0:T(8,128)(2,1)}), bf16[8,64,1024]{2,1,0:T(8,128)(2,1)S(1)}, u32[]{:S(2)}, u32[]{:S(2)}) async-start(bf16[8,64,1024]{2,1,0:T(8,128)(2,1)} %bitcast.42), calls=%async_computation.5 | async-start | bytes 2097152 | tf_op jit(solution)/shard_map/all_to_all | solution.py:69
Sparse Core Ops, SparseCore 0:
  93.6 76.4 reduce-scatter.2
  273.5 74.8 reduce-scatter.4
